TPU v7x, 32 devices: a whole 2x2x4 slice. The times are simulated.
32 devices in a mesh: groups: 2 (over x), elem: 16 (over z, y, core).
Axes of the slice: x: 2, y: 2, z: 4, core: 2. Of those that a mesh axis runs over, the one named last changes fastest.
Arguments:
- snapshots: float32 [2, 4096, 16384], P(None, ('groups', 'elem')), parts along dimension 1, may hold values from -6 to 6
- delays: float32 [384, 2048], replicated, may hold values from -3 to 3
- element_order: int32 [4096], P('groups'), parts along dimension 0, may hold values from 0 to 2047, each once
- beam_table: int32 [512], P('groups'), parts along dimension 0, may hold values from 0 to 383
- band_len: int32 [8], replicated, may hold values from 1 to 4, 16 in all
Outputs:
- beams: float32 [16384, 2, 512], P('elem', None, 'groups'), parts along dimension 2
- power_db: float32 [8, 512], P(None, 'groups'), parts along dimension 1
There are 2 independent parts, one for each index of `groups`. A program takes and returns all parts, laid end to end along the dimension named above; an argument that names none is the same for every part. Nothing has to cross between parts.
Inputs may be any that keep to these rules, and one draw needn't show every extreme that they name: `element_order`: each of 0 to 2047 appears once. `band_len`: the entries sum to 16.
All inputs are finite; a program needn't handle non-finite values.
Results may differ from a plain program's by a relative error of at most 0.0003.
Values sent between devices are 32-bit elements; how exact they have to be, the bound alone decides.
A program may use at most 128 MiB of HBM per device.

v0:
```python
import math
import jax
import jax.numpy as jnp
from jax import lax
from jax.sharding import PartitionSpec as P

epsilon = 1e-06


def band_of(band_len, position, unit_count):
    band_ends = jnp.cumsum(band_len)
    band_index = jnp.sum((band_ends <= position).astype(jnp.int32))
    selector = jnp.arange(band_len.shape[0], dtype=jnp.int32) == band_index
    band_size = jnp.sum(jnp.where(selector, band_len, 0))
    band_start = jnp.sum(jnp.where(selector, band_ends, 0)) - band_size
    frequency = (band_start.astype(jnp.float32) + 0.5 * band_size.astype(jnp.float32)) / float(
        unit_count
    )
    return (frequency, band_size, selector.astype(jnp.float32))


def steering(delays, element_order, beam_table, frequency):
    delay_rows = jnp.take(delays, beam_table, axis=0)
    delay_rows = jnp.take(delay_rows, element_order, axis=1)
    phases = 2.0 * math.pi * frequency * delay_rows
    scaling = float(delays.shape[1]) ** (-0.5)
    cosines = jnp.cos(phases) * scaling
    sines = -jnp.sin(phases) * scaling
    upper_rows = jnp.concatenate([cosines.T, sines.T], axis=1)
    lower_rows = jnp.concatenate([-sines.T, cosines.T], axis=1)
    return jnp.concatenate([upper_rows, lower_rows], axis=0)


def project(arrived, weights):
    columns = arrived.shape[2]
    stacked = arrived.reshape(2 * arrived.shape[1], columns)
    return lax.dot_general(
        stacked,
        weights,
        (((0,), (0,)), ((), ())),
        precision=lax.Precision.HIGHEST,
        preferred_element_type=jnp.float32,
    )


def local(snapshots, delays, element_order, beam_table, band_len):
    unit_count = lax.axis_size("elem")
    position = lax.axis_index("elem")
    frequency, band_size, selector = band_of(band_len, position, unit_count)
    weights = steering(delays, element_order, beam_table, frequency)
    beam_count = beam_table.shape[0]
    local_elems = snapshots.shape[1]
    unit_cols = snapshots.shape[2] // unit_count
    divided = snapshots.reshape(2, local_elems, unit_count, unit_cols)
    pieces = lax.all_to_all(divided, "elem", split_axis=2, concat_axis=1, tiled=True)
    formed = project(pieces.reshape(2, pieces.shape[1], pieces.shape[3]), weights)
    column_count = formed.shape[0]
    squares = jnp.sum(formed * formed, axis=0)
    power_mean = (squares[:beam_count] + squares[beam_count:]) / (
        band_size.astype(jnp.float32) * column_count
    )
    partial_value = selector[:, None] * power_mean[None, :]
    summed = lax.psum(partial_value, "elem")
    decibels = 10.0 * jnp.log10(summed + epsilon)
    return (formed.reshape(column_count, 2, beam_count), decibels)


def solution(mesh):
    return jax.shard_map(
        local,
        mesh=mesh,
        in_specs=(P(None, ("groups", "elem"), None), P(), P("groups"), P("groups"), P()),
        out_specs=(P("elem", None, "groups"), P(None, "groups")),
        check_vma=False,
    )
```

profile of v0, /device:TPU:0, one launch (start us, length us, event | category | flops | bytes accessed | tf_op | source)
XLA Modules:
  0.0 488.5 jit_solution(5320041055812886282)
XLA Ops:
  0.6 0.0 copy-start
  0.6 17.6 %copy.16 = f32[2,128,16384]{1,2,0:T(8,128)} copy(f32[2,128,16384]{2,1,0:T(8,128)} %param.5) | data formatting | bytes 33554432 | tf_op args[0]
  18.2 11.3 %copy.17 = f32[2,128,16,1024]{1,3,0,2:T(8,128)} copy(f32[2,128,16,1024]{1,3,2,0:T(8,128)} %bitcast.19) | data formatting | bytes 33554432 | tf_op jit(solution)/shard_map/reshape | solution.py:54
  29.5 0.0 copy-start.3
  29.5 7.6 %all-to-all-start = ((f32[2,128,16,1024]{1,3,0,2:T(8,128)}), f32[2,128,16,1024]{1,3,0,2:T(8,128)}, u32[]{:S(2)}, u32[]{:S(2)}) async-start(f32[2,128,16,1024]{1,3,0,2:T(8,128)} %copy.17), calls=%async_computation | async-start | bytes 33554432 | tf_op jit(solution)/shard_map/all_to_all | solution.py:55
  37.1 0.0 copy-done.3
  37.2 0.0 copy-done
  37.2 2.7 gather_fusion
  39.9 3.1 broadcast_select_fusion
  43.0 0.0 copy-start.4
  43.0 0.0 copy-start.2
  43.0 1.9 copy.15
  44.9 0.0 copy-done.4
  44.9 0.2 reduce-window.9
  45.1 0.6 fusion.10
  45.8 1.3 fusion.11
  49.1 0.0 copy-done.2
  49.1 8.6 %gather_fusion.1 = f32[2048,256]{1,0:T(8,128)} fusion(f32[256,2048]{0,1:T(8,128)S(1)} %copy.15, s32[2048]{0:T(1024)S(1)} %fusion.9), kind=kCustom, calls=%fused_computation.1 | custom fusion | bytes 4202496 | tf_op jit(solution)/shard_map/jit(_take)/gather | solution.py:24
  57.7 0.6 fusion.12
  58.4 10.9 %fusion.14 = (f32[2048,256]{1,0:T(8,128)S(1)}, f32[2048,256]{1,0:T(8,128)}, f32[2048,256]{1,0:T(8,128)}) fusion(f32[2048,256]{1,0:T(8,128)} %gather_fusion.1, pred[2048]{0:T(1024)(128)(4,1)S(1)} %compare_and_fusion, f32[]{:T(128)S(6)} %mul_shard_map.7), kind=kLoop, calls=%fused_computation.33 | loop fusion | flops 3145728 | bytes 8390660 | tf_op jit(solution)/shard_map/neg | solution.py:30
  69.3 264.4 %all-to-all-done = f32[2,128,16,1024]{1,3,0,2:T(8,128)} async-done(((f32[2,128,16,1024]{1,3,0,2:T(8,128)}), f32[2,128,16,1024]{1,3,0,2:T(8,128)}, u32[]{:S(2)}, u32[]{:S(2)}) %all-to-all-start) | async-done | bytes 16777248 | tf_op jit(solution)/shard_map/all_to_all | solution.py:55
  333.8 18.0 %copy.18 = f32[2,128,16,1024]{3,1,2,0:T(8,128)} copy(f32[2,128,16,1024]{1,3,0,2:T(8,128)} %all-to-all-done) | data formatting | bytes 33554432 | tf_op jit(solution)/shard_map/all_to_all | solution.py:55
  351.8 33.0 %fusion.8 = (f32[512]{0:T(512)S(1)}, f32[512,1024]{1,0:T(8,128)}) fusion(f32[4096,1024]{1,0:T(8,128)} %bitcast.20, f32[2048,256]{1,0:T(8,128)} %get-tuple-element.12, f32[2048,256]{1,0:T(8,128)S(1)} %get-tuple-element.10, f32[2048,256]{1,0:T(8,128)} %get-tuple-element.11), kind=kOutput, calls=%fused_computation.11 | convolution fusion | flops 25777143808 | bytes 25167872 | tf_op jit(solution)/shard_map/dot_general | solution.py:37
  384.7 0.0 copy-start.1
  384.7 4.3 copy.19
  389.0 0.1 broadcast_multiply_fusion
  389.1 98.8 %psum.7 = f32[8,256]{1,0:T(8,128)S(1)} all-reduce(f32[8,256]{1,0:T(8,128)S(1)} %broadcast_multiply_fusion), channel_id=1, replica_groups=mesh['groups'=2,'elem'=16] {'elem'}, use_global_device_ids=true, to_apply=%region_5.6 | all-reduce | flops 2048 | bytes 16384 | tf_op jit(solution)/shard_map/psum | solution.py:63
  487.9 0.6 log_multiply_fusion
  488.5 0.0 copy-done.1
  (6 shorter events, 0.0 us)
Async XLA Ops:
  0.6 36.5 %copy-start = (f32[384,2048]{1,0:T(8,128)S(1)}, f32[384,2048]{1,0:T(8,128)}, u32[]{:S(2)}) copy-start(f32[384,2048]{1,0:T(8,128)} %param.6) | copy-start | bytes 9437188
  29.5 7.6 %copy-start.3 = (s32[256]{0:T(256)S(1)}, s32[256]{0:T(256)}, u32[]{:S(2)}) copy-start(s32[256]{0:T(256)} %param.8) | copy-start | bytes 3076
  29.5 304.2 %all-to-all-start = ((f32[2,128,16,1024]{1,3,0,2:T(8,128)}), f32[2,128,16,1024]{1,3,0,2:T(8,128)}, u32[]{:S(2)}, u32[]{:S(2)}) async-start(f32[2,128,16,1024]{1,3,0,2:T(8,128)} %copy.17), calls=%async_computation | async-start | bytes 33554432 | tf_op jit(solution)/shard_map/all_to_all | solution.py:55
  43.0 2.0 copy-start.4
  43.0 6.1 %copy-start.2 = (s32[2048]{0:T(1024)S(1)}, s32[2048]{0:T(1024)}, u32[]{:S(2)}) copy-start(s32[2048]{0:T(1024)} %param.7) | copy-start | bytes 24580
  384.7 103.8 %copy-start.1 = (f32[384,2048]{1,0:T(8,128)S(1)}, f32[384,2048]{1,0:T(8,128)}, u32[]{:S(2)}) copy-start(f32[384,2048]{1,0:T(8,128)} %param.6) | copy-start | bytes 9437188
where the time goes:
time: 489 us; the launch traced here: 488 us
  waiting for transfers between devices  264 us (54%)
  blocking collectives  98.8 us (20%)
  local copies, waits for them, and re-layouts  64.4 us (13%)
  matrix products  33 us (7%)
  other arithmetic  17.6 us (4%)
  starting transfers between devices  7.6 us (2%)
    all_to_all x1, waiting for transfers between devices, local(): lax.all_to_all(divided, 'elem', split_axis=2, concat_axis=1, tiled=True)  264 us
    psum x1, blocking collectives, local(): summed = lax.psum(partial_value, 'elem')  98.8 us
    dot_general x1, matrix products, project(): lax.dot_general(stacked, weights, (((0,), (0,)), ((), ())), precision=lax...  33 us
    unnamed x12, local copies, waits for them, and re-layouts  21.9 us
    all_to_all x1, local copies, waits for them, and re-layouts, local(): lax.all_to_all(divided, 'elem', split_axis=2, concat_axis=1, tiled=True)  18 us
    reshape x1, local copies, waits for them, and re-layouts, local(): divided = snapshots.reshape(2, local_elems, unit_count, unit_cols)  11.3 us
    neg x1, other arithmetic, steering(): lower_rows = jnp.concatenate([-sines.T, cosines.T], axis=1)  10.9 us
  transfers between devices with their start and end apart: 1, of which 1 were waited for; matrix products, arithmetic and copies ran while one was open for 6% of the time, Pallas kernels for 0%

commit v1 on v0

--- a/solution.py
+++ b/solution.py
@@ -52,7 +52,10 @@
     local_elems = snapshots.shape[1]
     unit_cols = snapshots.shape[2] // unit_count
     divided = snapshots.reshape(2, local_elems, unit_count, unit_cols)
-    pieces = lax.all_to_all(divided, "elem", split_axis=2, concat_axis=1, tiled=True)
+    pieces = jnp.concatenate(
+        lax.all_to_all(jnp.stack(jnp.split(divided, lax.axis_size("elem"), axis=2)), "elem", 0, 0),
+        axis=1,
+    )
     formed = project(pieces.reshape(2, pieces.shape[1], pieces.shape[3]), weights)
     column_count = formed.shape[0]
     squares = jnp.sum(formed * formed, axis=0)

time: 489 us -> 507 us (1.037)
  local copies, waits for them, and re-layouts: 64.4 us -> 83.8 us
    unnamed x12 -> x27, local copies, waits for them, and re-layouts: 21.9 us -> 49 us
    all_to_all x1 -> x0, local copies, waits for them, and re-layouts: 18 us -> none  [local(): lax.all_to_all(divided, 'elem', split_axis=2, concat_axis=1, tiled=True)]
    reshape x1, local copies, waits for them, and re-layouts: 11.3 us -> 18 us  [local(): jnp.concatenate(lax.all_to_all(jnp.stack(jnp.split(divided, lax.axis_size...]
where the time goes in v1:
time: 507 us; the launch traced here: 506 us
  waiting for transfers between devices  262 us (52%)
  blocking collectives  98.8 us (19%)
  local copies, waits for them, and re-layouts  83.8 us (17%)
  matrix products  33.2 us (7%)
  other arithmetic  17.7 us (3%)
  starting transfers between devices  7.6 us (1%)
    all_to_all x1, waiting for transfers between devices, local(): lax.all_to_all(jnp.stack(jnp.split(divided, lax.axis_size('elem'), axis=2...  262 us
    psum x1, blocking collectives, local(): summed = lax.psum(partial_value, 'elem')  98.8 us
    unnamed x27, local copies, waits for them, and re-layouts  49 us
    dot_general x1, matrix products, project(): lax.dot_general(stacked, weights, (((0,), (0,)), ((), ())), precision=lax...  33.2 us
    reshape x1, local copies, waits for them, and re-layouts, local(): jnp.concatenate(lax.all_to_all(jnp.stack(jnp.split(divided, lax.axis_size...  18 us
    neg x1, other arithmetic, steering(): lower_rows = jnp.concatenate([-sines.T, cosines.T], axis=1)  11.1 us
    gather x1, local copies, waits for them, and re-layouts, steering(): delay_rows = jnp.take(delay_rows, element_order, axis=1)  10.2 us
  transfers between devices with their start and end apart: 1, of which 1 were waited for; matrix products, arithmetic and copies ran while one was open for 6% of the time, Pallas kernels for 0%

profile of v1, /device:TPU:0, one launch (start us, length us, event | category | flops | bytes accessed | tf_op | source)
XLA Modules:
  0.0 505.7 jit_solution(16571479017267385593)
XLA Ops:
  0.6 0.0 copy-start
  0.6 17.6 %copy.26 = f32[2,128,16384]{1,2,0:T(8,128)} copy(f32[2,128,16384]{2,1,0:T(8,128)} %param.5) | data formatting | bytes 33554432 | tf_op args[0]
  18.2 0.0 copy-start.1
  18.2 2.4 fusion.23
  20.6 3.1 fusion.22
  23.7 2.9 fusion.21
  26.6 2.3 fusion.20
  28.9 2.3 fusion.19
  31.2 2.3 fusion.18
  33.5 2.3 fusion.17
  35.8 2.3 fusion.16
  38.1 0.0 copy-done.1
  38.1 1.1 fusion.15
  39.2 1.0 fusion.14
  40.2 1.0 fusion.13
  41.3 1.0 fusion.12
  42.3 1.1 fusion.11
  43.4 1.0 fusion.10
  44.5 1.0 fusion.9
  45.5 1.1 fusion.8
  46.6 0.0 copy-start.4
  46.6 0.0 copy-start.3
  46.6 7.6 %all-to-all-start = ((f32[16,2,128,1,1024]{2,4,1,3,0:T(8,128)}), f32[16,2,128,1,1024]{2,4,1,3,0:T(8,128)}, u32[]{:S(2)}, u32[]{:S(2)}) async-start(f32[16,2,128,1,1024]{2,4,1,3,0:T(8,128)} %fusion.8), calls=%async_computation | async-start | bytes 33554432 | tf_op jit(solution)/shard_map/all_to_all | solution.py:56
  54.2 0.0 copy-start.2
  54.2 0.0 copy-done.4
  54.2 0.2 reduce-window.9
  54.4 0.6 fusion.25
  55.0 1.3 fusion.26
  58.4 0.0 copy-done.3
  58.4 0.0 copy-done
  58.4 2.7 gather_fusion
  61.1 3.1 broadcast_select_fusion
  64.2 2.9 copy.43
  67.1 0.0 copy-done.2
  67.2 10.2 %gather_fusion.1 = f32[2048,256]{1,0:T(8,128)} fusion(f32[256,2048]{0,1:T(8,128)} %copy.43, s32[2048]{0:T(1024)S(1)} %fusion.24), kind=kCustom, calls=%fused_computation.1 | custom fusion | bytes 4202496 | tf_op jit(solution)/shard_map/jit(_take)/gather | solution.py:24
  77.3 0.6 fusion.27
  78.0 11.1 %fusion.29 = (f32[2048,256]{1,0:T(8,128)}, f32[2048,256]{1,0:T(8,128)}, f32[2048,256]{1,0:T(8,128)}) fusion(f32[2048,256]{1,0:T(8,128)} %gather_fusion.1, pred[2048]{0:T(1024)(128)(4,1)S(1)} %compare_and_fusion, f32[]{:T(128)S(6)} %mul_shard_map.7), kind=kLoop, calls=%fused_computation.64 | loop fusion | flops 3145728 | bytes 8390660 | tf_op jit(solution)/shard_map/neg | solution.py:30
  89.1 261.7 %all-to-all-done = f32[16,2,128,1,1024]{2,4,1,3,0:T(8,128)} async-done(((f32[16,2,128,1,1024]{2,4,1,3,0:T(8,128)}), f32[16,2,128,1,1024]{2,4,1,3,0:T(8,128)}, u32[]{:S(2)}, u32[]{:S(2)}) %all-to-all-start) | async-done | bytes 16777248 | tf_op jit(solution)/shard_map/all_to_all | solution.py:56
  350.8 18.0 %copy.42 = f32[2,16,128,1,1024]{4,2,1,0,3:T(8,128)} copy(f32[2,16,128,1,1024]{2,4,0,3,1:T(8,128)} %bitcast.17) | data formatting | bytes 33554432 | tf_op jit(solution)/shard_map/reshape | solution.py:55
  368.8 33.2 %multiply_reduce_fusion = (f32[512]{0:T(512)S(1)}, f32[1024,512]{0,1:T(8,128)}) fusion(f32[4096,1024]{1,0:T(8,128)} %bitcast.121, f32[2048,256]{1,0:T(8,128)} %get-tuple-element.10, f32[2048,256]{1,0:T(8,128)} %get-tuple-element.8, f32[2048,256]{1,0:T(8,128)} %get-tuple-element.9), kind=kOutput, calls=%fused_computation.13 | convolution fusion | flops 25777143808 | bytes 25167872 | tf_op jit(solution)/shard_map/dot_general | solution.py:37
  402.1 4.1 copy.44
  406.2 0.1 broadcast_multiply_fusion
  406.3 98.8 %psum.7 = f32[8,256]{1,0:T(8,128)S(1)} all-reduce(f32[8,256]{1,0:T(8,128)S(1)} %broadcast_multiply_fusion), channel_id=1, replica_groups=mesh['groups'=2,'elem'=16] {'elem'}, use_global_device_ids=true, to_apply=%region_5.6 | all-reduce | flops 2048 | bytes 16384 | tf_op jit(solution)/shard_map/psum | solution.py:66
  505.1 0.6 log_multiply_fusion
  (6 shorter events, 0.0 us)
Async XLA Ops:
  0.6 57.8 %copy-start = (f32[384,2048]{1,0:T(8,128)S(1)}, f32[384,2048]{1,0:T(8,128)}, u32[]{:S(2)}) copy-start(f32[384,2048]{1,0:T(8,128)} %param.6) | copy-start | bytes 9437188
  18.2 19.9 %copy-start.1 = (f32[2,128,16384]{1,2,0:T(8,128)S(1)}, f32[2,128,16384]{1,2,0:T(8,128)}, u32[]{:S(2)}) copy-start(f32[2,128,16384]{1,2,0:T(8,128)} %copy.26) | copy-start | bytes 50331652
  46.6 7.6 %copy-start.4 = (s32[8]{0:T(128)S(1)}, s32[8]{0:T(128)}, u32[]{:S(2)}) copy-start(s32[8]{0:T(128)} %param.9) | copy-start | bytes 100
  46.6 11.8 %copy-start.3 = (s32[256]{0:T(256)S(1)}, s32[256]{0:T(256)}, u32[]{:S(2)}) copy-start(s32[256]{0:T(256)} %param.8) | copy-start | bytes 3076
  46.6 304.2 %all-to-all-start = ((f32[16,2,128,1,1024]{2,4,1,3,0:T(8,128)}), f32[16,2,128,1,1024]{2,4,1,3,0:T(8,128)}, u32[]{:S(2)}, u32[]{:S(2)}) async-start(f32[16,2,128,1,1024]{2,4,1,3,0:T(8,128)} %fusion.8), calls=%async_computation | async-start | bytes 33554432 | tf_op jit(solution)/shard_map/all_to_all | solution.py:56
  54.2 12.9 %copy-start.2 = (s32[2048]{0:T(1024)S(1)}, s32[2048]{0:T(1024)}, u32[]{:S(2)}) copy-start(s32[2048]{0:T(1024)} %param.7) | copy-start | bytes 24580
